TPU v7x, 32 devices: a whole 2x2x4 slice. The times are simulated.
32 devices in a mesh: parts: 2 (over y), leaf: 4 (over z), mid: 2 (over x), top: 2 (over core).
Axes of the slice: x: 2, y: 2, z: 4, core: 2. Of those that a mesh axis runs over, the one named last changes fastest.
Arguments:
- leaf_precision: float32 [8, 2, 2, 128, 128], P(('parts', 'leaf'), 'mid', 'top'), parts along dimension 0, may hold values from -40 to 40, as said below
- basis_fine: float32 [8, 2, 2, 128, 128], P(('parts', 'leaf'), 'mid', 'top'), parts along dimension 0, may hold values from -1 to 1
- basis_mid: float32 [8, 2, 2, 128, 128], P(('parts', 'leaf'), 'mid', 'top'), parts along dimension 0, may hold values from -1 to 1
- basis_coarse: float32 [8, 2, 2, 128, 128], P(('parts', 'leaf'), 'mid', 'top'), parts along dimension 0, may hold values from -1 to 1
- core_fine: float32 [128, 128], replicated, may hold values from -20 to 20, as said below
- core_mid: float32 [128, 128], replicated, may hold values from -20 to 20, as said below
- core_coarse: float32 [128, 128], replicated, may hold values from -20 to 20, as said below
- observations: float32 [8, 2, 2, 128, 128], P(('parts', 'leaf'), 'mid', 'top'), parts along dimension 0, may hold values from -20 to 20
Outputs:
- solution: float32 [8, 2, 2, 128, 128], P(('parts', 'leaf'), 'mid', 'top'), parts along dimension 0
There are 2 independent parts, one for each index of `parts`. A program takes and returns all parts, laid end to end along the dimension named above; an argument that names none is the same for every part. Nothing has to cross between parts.
Inputs may be any that keep to these rules, and one draw needn't show every extreme that they name: Every leaf_precision[l, m, t] is symmetric positive definite. `core_fine`: symmetric positive definite. `core_mid`: symmetric positive definite. `core_coarse`: symmetric positive definite.
All inputs are finite; a program needn't handle non-finite values.
Results may differ from a plain program's by a relative error of at most 0.00005.
Values sent between devices are 32-bit elements; how exact they have to be, the bound alone decides.
A program may use at most 64 MiB of HBM per device.

v0:
```python
import jax
import jax.numpy as jnp
from jax import lax
from jax.sharding import PartitionSpec as P


def solve_core(matrix, right_side):
    return jax.scipy.linalg.cho_solve((jnp.linalg.cholesky(matrix), True), right_side)


def cross_dot(left_hand, right_side):
    return jnp.dot(left_hand.T, right_side, precision=lax.Precision.HIGHEST)


def plain_dot(left_hand, right_side):
    return jnp.dot(left_hand, right_side, precision=lax.Precision.HIGHEST)


def local(
    leaf_precision,
    basis_fine,
    basis_mid,
    basis_coarse,
    core_fine,
    core_mid,
    core_coarse,
    observations,
):
    fine_basis = basis_fine[0, 0, 0]
    mid_basis = basis_mid[0, 0, 0]
    coarse_basis = basis_coarse[0, 0, 0]
    core_rank = fine_basis.shape[1]
    stacked = jnp.concatenate([fine_basis, mid_basis, coarse_basis, observations[0, 0, 0]], axis=1)
    solved = plain_dot(leaf_precision[0, 0, 0], stacked)
    fine_part = cross_dot(fine_basis, solved)
    mid_part = cross_dot(mid_basis, solved[:, core_rank:])
    coarse_part = cross_dot(coarse_basis, solved[:, 2 * core_rank :])
    fine_gram, mid_part, coarse_part = lax.psum((fine_part, mid_part, coarse_part), "leaf")
    fine_coef = solve_core(core_fine + fine_gram[:, :core_rank], fine_gram[:, core_rank:])
    mid_part = mid_part - cross_dot(fine_gram[:, core_rank : 2 * core_rank], fine_coef)
    coarse_part = coarse_part - cross_dot(
        fine_gram[:, 2 * core_rank : 3 * core_rank], fine_coef[:, core_rank:]
    )
    mid_gram, coarse_part = lax.psum((mid_part, coarse_part), "mid")
    mid_coef = solve_core(core_mid + mid_gram[:, :core_rank], mid_gram[:, core_rank:])
    coarse_part = coarse_part - cross_dot(mid_gram[:, core_rank : 2 * core_rank], mid_coef)
    coarse_gram = lax.psum(coarse_part, "top")
    coarse_coef = solve_core(core_coarse + coarse_gram[:, :core_rank], coarse_gram[:, core_rank:])
    after_fine = solved[:, core_rank:] - plain_dot(solved[:, :core_rank], fine_coef)
    after_mid = after_fine[:, core_rank:] - plain_dot(after_fine[:, :core_rank], mid_coef)
    answer = after_mid[:, core_rank:] - plain_dot(after_mid[:, :core_rank], coarse_coef)
    return answer[None, None, None]


def solution(mesh):
    placed = (
        P(("parts", "leaf"), "mid", "top", None, None),
        P(("parts", "leaf"), "mid", "top", None, None),
        P(("parts", "leaf"), "mid", "top", None, None),
        P(("parts", "leaf"), "mid", "top", None, None),
        P(),
        P(),
        P(),
        P(("parts", "leaf"), "mid", "top", None, None),
    )
    return jax.shard_map(
        local,
        mesh=mesh,
        in_specs=placed,
        out_specs=P(("parts", "leaf"), "mid", "top", None, None),
        check_vma=False,
    )
```

profile of v0, /device:TPU:0, one launch (start us, length us, event | category | flops | bytes accessed | tf_op | source)
XLA Modules:
  0.0 182.1 jit_solution(10477967677573952904)
XLA Ops:
  6.5 0.0 copy-start
  6.5 0.0 all-reduce.8.cloned.1.call-start
  6.5 0.8 copy-done
  7.4 1.6 fusion.1
  8.9 0.0 copy-done.3
  8.9 0.0 copy-start.4
  9.0 1.0 convolution_bitcast_fusion.1
  9.9 0.0 copy-done.4
  9.9 0.9 convolution_bitcast_fusion.2
  10.9 0.0 copy-done.5
  10.9 1.1 convolution_bitcast_fusion
  11.9 0.0 all-reduce.8.cloned.1.call-update
  11.9 0.0 all-reduce.10.cloned.1.call-start
  12.0 0.8 copy-done.10
  12.8 0.1 copy.9
  12.9 41.6 %all-reduce.8.cloned.1.call-done = (f32[128,256]{0,1:T(8,128)}, f32[128,512]{0,1:T(8,128)}, f32[128,384]{0,1:T(8,128)}) async-done(((f32[128,256]{0,1:T(8,128)}, f32[128,512]{0,1:T(8,128)}, f32[128,384]{0,1:T(8,128)}), (f32[128,256]{0,1:T(8,128)}, f32[128,512]{0,1:T(8,128)}, f32[128,384]{0,1:T(8,128)})) %all-reduce.8.cloned.1.call-update) | async-done | bytes 589840 | tf_op jit(solution)/shard_map/psum | solution.py:38
  54.4 0.8 slice_add_fusion.2
  55.3 0.1 copy.10
  55.4 11.7 %cholesky.59 = f32[128,128]{1,0:T(8,128)S(1)} custom-call(f32[128,128]{1,0:T(8,128)S(1)} %fusion.38), custom_call_target="Cholesky" | custom-call | tf_op jit(solution)/shard_map/jit(cholesky)/cholesky | solution.py:8
  67.2 0.6 compare_reduce_fusion.2
  67.8 0.7 fusion.16
  68.5 9.8 %custom-call.23 = f32[1,128,128]{1,2,0:T(8,128)S(1)} custom-call(f32[1,128,128]{2,1,0:T(8,128)S(1)} %fusion.16), custom_call_target="InvertDiagBlocksLowerTriangular" | custom-call | tf_op jit(solution)/shard_map/jit(_cho_solve)/triangular_solve | solution.py:8
  78.3 0.0 copy-done.1
  78.3 0.4 fusion.9
  78.7 0.0 copy-start.6
  78.7 0.3 fusion.35
  79.0 0.6 copy-done.6
  79.6 1.2 convolution_subtract_fusion
  80.8 0.0 copy-done.8
  80.8 1.0 convolution_subtract_fusion.3
  81.8 0.0 all-reduce.10.cloned.1.call-update
  81.9 0.0 copy-start.12
  81.9 0.2 all-reduce.6.cloned.1.call-start
  82.1 0.6 copy-done.11
  82.7 0.1 copy.13
  82.8 0.0 copy-done.12
  82.8 0.1 copy.18
  82.9 0.5 convolution_subtract_fusion.1
  83.4 22.6 %all-reduce.10.cloned.1.call-done = (f32[128,256]{0,1:T(8,128)}, f32[128,384]{0,1:T(8,128)}) async-done(((f32[128,256]{0,1:T(8,128)}, f32[128,384]{0,1:T(8,128)}), (f32[128,256]{0,1:T(8,128)}, f32[128,384]{0,1:T(8,128)})) %all-reduce.10.cloned.1.call-update) | async-done | bytes 327696 | tf_op jit(solution)/shard_map/psum | solution.py:44
  105.9 0.8 slice_add_fusion.1
  106.8 0.1 copy.14
  106.9 0.0 copy-start.2
  106.9 11.7 %cholesky.70 = f32[128,128]{1,0:T(8,128)S(1)} custom-call(f32[128,128]{1,0:T(8,128)S(1)} %fusion.34), custom_call_target="Cholesky" | custom-call | tf_op jit(solution)/shard_map/jit(cholesky)/cholesky | solution.py:8
  118.7 0.6 compare_reduce_fusion.1
  119.3 0.7 fusion.17
  120.0 9.8 %custom-call.24 = f32[1,128,128]{1,2,0:T(8,128)S(1)} custom-call(f32[1,128,128]{2,1,0:T(8,128)S(1)} %fusion.17), custom_call_target="InvertDiagBlocksLowerTriangular" | custom-call | tf_op jit(solution)/shard_map/jit(_cho_solve)/triangular_solve | solution.py:8
  129.8 0.0 copy-done.2
  129.8 0.3 fusion.14
  130.1 0.3 fusion.31
  130.4 0.6 copy-done.7
  131.0 1.0 convolution_subtract_fusion.2
  132.1 0.0 all-reduce.6.cloned.1.call-update
  132.1 0.4 convolution_subtract_fusion.4
  132.5 17.7 %all-reduce.6.cloned.1.call-done = f32[128,256]{0,1:T(8,128)} async-done(((f32[128,256]{0,1:T(8,128)}), f32[128,256]{0,1:T(8,128)}) %all-reduce.6.cloned.1.call-update) | async-done | bytes 131088 | tf_op jit(solution)/shard_map/psum | solution.py:47
  150.2 0.8 slice_add_fusion
  151.0 0.1 copy.19
  151.1 11.7 %cholesky.81 = f32[128,128]{1,0:T(8,128)S(1)} custom-call(f32[128,128]{1,0:T(8,128)S(1)} %fusion.30), custom_call_target="Cholesky" | custom-call | tf_op jit(solution)/shard_map/jit(cholesky)/cholesky | solution.py:8
  162.9 0.6 compare_reduce_fusion
  163.5 0.7 fusion.18
  164.2 9.8 %custom-call.25 = f32[1,128,128]{1,2,0:T(8,128)S(1)} custom-call(f32[1,128,128]{2,1,0:T(8,128)S(1)} %fusion.18), custom_call_target="InvertDiagBlocksLowerTriangular" | custom-call | tf_op jit(solution)/shard_map/jit(_cho_solve)/triangular_solve | solution.py:8
  174.0 0.3 fusion.19
  174.3 0.2 fusion.27
  174.5 0.3 fusion
  174.8 0.7 copy.21
  (15 shorter events, 0.2 us)
Async XLA Ops:
  6.5 0.8 copy-start
  6.5 47.9 %all-reduce.8.cloned.1.call-start = ((), (), s32[]{:S(2)}) async-start(), calls=%async_computation.1 | async-start | bytes 1179648 | tf_op jit(solution)/shard_map/psum | solution.py:38
  7.4 1.6 copy-start.3
  8.9 1.0 copy-start.4
  9.9 0.9 copy-start.5
  11.9 0.8 copy-start.10
  11.9 94.0 %all-reduce.10.cloned.1.call-start = ((), (), s32[]{:S(2)}) async-start(), calls=%async_computation.2 | async-start | bytes 655360 | tf_op jit(solution)/shard_map/psum | solution.py:44
  55.3 23.0 %copy-start.1 = (f32[128,512]{0,1:T(8,128)S(1)}, f32[128,512]{0,1:T(8,128)}, u32[]{:S(2)}) copy-start(f32[128,512]{0,1:T(8,128)} %get-tuple-element.7) | copy-start | bytes 786436
  78.7 0.9 copy-start.6
  79.6 1.2 copy-start.8
  81.8 0.8 copy-start.11
  81.9 0.9 copy-start.12
  81.9 68.3 %all-reduce.6.cloned.1.call-start = ((), (), s32[]{:S(2)}) async-start(), calls=%async_computation | async-start | bytes 262144 | tf_op jit(solution)/shard_map/psum | solution.py:47
  106.9 22.9 %copy-start.2 = (f32[128,384]{0,1:T(8,128)S(1)}, f32[128,384]{0,1:T(8,128)}, u32[]{:S(2)}) copy-start(f32[128,384]{0,1:T(8,128)} %get-tuple-element.10) | copy-start | bytes 589828
  130.1 0.9 copy-start.7
  151.1 22.9 %copy-start.9 = (f32[128,256]{0,1:T(8,128)S(1)}, f32[128,256]{0,1:T(8,128)}, u32[]{:S(2)}) copy-start(f32[128,256]{0,1:T(8,128)} %all-reduce.6.cloned.1.call-done) | copy-start | bytes 393220
Sparse Core Ops, SparseCore 0:
  12.1 42.3 all-reduce.7
  82.0 23.9 all-reduce.9
  132.2 17.9 all-reduce.5
where the time goes:
time: 183 us; the launch traced here: 182 us
  waiting for transfers between devices  81.9 us (45%)
  other arithmetic  71.1 us (39%)
  between operations  13.4 us (7%)
  matrix products  10.7 us (6%)
  local copies, waits for them, and re-layouts  4.69 us (3%)
    psum x1, waiting for transfers between devices, local(): lax.psum((fine_part, mid_part, coarse_part), 'leaf')  41.6 us
    another operation x9, other arithmetic, solve_core(): jnp.linalg.cholesky(matrix)  37.2 us
    another operation x6, other arithmetic, solve_core(): jax.scipy.linalg.cho_solve((jnp.linalg.cholesky(matrix), True), right_side)  31.4 us
    psum x1, waiting for transfers between devices, local(): mid_gram, coarse_part = lax.psum((mid_part, coarse_part), 'mid')  22.6 us
    psum x1, waiting for transfers between devices, local(): coarse_gram = lax.psum(coarse_part, 'top')  17.7 us
    dot_general x6, matrix products, cross_dot(): return jnp.dot(left_hand.T, right_side, precision=lax.Precision.HIGHEST)  6.2 us
    unnamed x29, local copies, waits for them, and re-layouts  3.7 us
  transfers between devices with their start and end apart: 3, of which 3 were waited for; matrix products, arithmetic and copies ran while one was open for 1% of the time, Pallas kernels for 0%

commit v1 on v0

v1 whole, which is shorter than its diff:
```python
import functools

import jax
import jax.numpy as jnp
from jax import lax
from jax.experimental import pallas as pl
from jax.experimental.pallas import tpu as pltpu
from jax.sharding import PartitionSpec as P

MESH = pl.DeviceIdType.MESH
PANEL = 8


def dot(left_hand, right_side):
    return jnp.dot(
        left_hand, right_side, precision=lax.Precision.HIGHEST, preferred_element_type=jnp.float32
    )


def split3(x):
    high = x.astype(jnp.bfloat16).astype(jnp.float32)
    rest = x - high
    mid = rest.astype(jnp.bfloat16).astype(jnp.float32)
    low = (rest - mid).astype(jnp.bfloat16).astype(jnp.float32)
    return high, mid, low


def rank_update(panel, scaled):
    p1, p2, p3 = split3(panel)
    r1, r2, r3 = split3(scaled)
    left_hand = jnp.concatenate([p1, p1, p2, p2, p1, p3], axis=0).T.astype(jnp.bfloat16)
    right_side = jnp.concatenate([r1, r2, r1, r2, r3, r1], axis=0).astype(jnp.bfloat16)
    return jnp.dot(left_hand, right_side, preferred_element_type=jnp.float32)


def negated_inverse(a_ref, matrix):
    size = matrix.shape[0]
    zero = jnp.zeros((PANEL, size), jnp.float32)
    a_ref[pl.ds(0, PANEL), :] = zero
    a_ref[pl.ds(PANEL, size), :] = matrix
    a_ref[pl.ds(PANEL + size, PANEL), :] = zero
    lane = lax.broadcasted_iota(jnp.int32, (PANEL, size), 1)
    sub = lax.broadcasted_iota(jnp.int32, (PANEL, size), 0)
    lane_full = lax.broadcasted_iota(jnp.int32, (size, size), 1)

    def columns(block, k):
        return [
            jnp.broadcast_to(
                jnp.sum(jnp.where(lane == k * PANEL + j, block, 0.0), axis=1, keepdims=True),
                block.shape,
            )
            for j in range(PANEL)
        ]

    def apply(k, panel, scaled):
        inside = (lane_full >= k * PANEL) & (lane_full < (k + 1) * PANEL)
        current = a_ref[pl.ds(PANEL, size), :]
        a_ref[pl.ds(PANEL, size), :] = jnp.where(inside, 0.0, current) - rank_update(panel, scaled)
        a_ref[pl.ds(pl.multiple_of((k + 1) * PANEL, PANEL), PANEL), :] = scaled

    def body(k, carry):
        panel_before, scaled_before, panel = carry
        apply(k - 1, panel_before, scaled_before)
        inside = (lane >= k * PANEL) & (lane < (k + 1) * PANEL)
        cols = columns(panel, k)
        x = jnp.where(inside, jnp.where(lane - k * PANEL == sub, 1.0, 0.0), panel)
        for i in range(PANEL):
            pivot = 1.0 / jnp.broadcast_to(cols[i][i : i + 1], x.shape)
            here = sub == i

            def step(v):
                row = jnp.broadcast_to(v[i : i + 1], v.shape) * pivot
                return jnp.where(here, row, v - cols[i] * row)

            x_new = step(x)
            for j in range(i + 1, PANEL):
                cols[j] = step(cols[j])
            x = x_new
        scaled = jnp.where(inside, -x, x)
        following = a_ref[pl.ds(pl.multiple_of((k + 2) * PANEL, PANEL), PANEL), :]
        coefs = columns(following, k)
        panel_next = jnp.where(inside, 0.0, following)
        for j in range(PANEL):
            panel_next = panel_next - coefs[j] * jnp.broadcast_to(scaled[j : j + 1], x.shape)
        return panel, scaled, panel_next

    steps = size // PANEL
    panel, scaled, _ = lax.fori_loop(0, steps, body, (zero, zero, matrix[:PANEL]))
    apply(steps - 1, panel, scaled)
    return a_ref[pl.ds(PANEL, size), :]


def kernel(
    n_leaf, n_mid, n_top,
    prec_ref, fine_ref, mid_ref, coarse_ref, core_fine_ref, core_mid_ref, core_coarse_ref, obs_ref,
    out_ref,
    a_ref, ff_ref, ff_in, bulk_ref, rs_in, ag_ref, piece_ref, piece_in, quarter_ref, s_ref,
    top_ref, top_in,
    ff_send, ff_recv, rs_send, rs_recv, ag_send, ag_recv, mid_send, mid_recv,
    s_send, s_recv, top_send, top_recv,
):
    r = fine_ref.shape[1]
    rows = r // n_leaf
    leaf, mid, top = lax.axis_index("leaf"), lax.axis_index("mid"), lax.axis_index("top")
    barrier = pltpu.get_barrier_semaphore()

    def peer(axis, index, count, step):
        return {axis: lax.rem(index + step, count)}

    for axis, index, count in (("leaf", leaf, n_leaf), ("mid", mid, n_mid), ("top", top, n_top)):
        for step in range(1, count):
            pl.semaphore_signal(
                barrier, inc=1, device_id=peer(axis, index, count, step), device_id_type=MESH
            )

    def send(src, dst, send_sem, recv_sem, axis, index, count, step):
        copy = pltpu.make_async_remote_copy(
            src_ref=src, dst_ref=dst, send_sem=send_sem.at[step - 1], recv_sem=recv_sem.at[step - 1],
            device_id=peer(axis, index, count, step), device_id_type=MESH,
        )
        copy.start()
        return copy

    prec = prec_ref[...]
    fine, middle, coarse = fine_ref[...], mid_ref[...], coarse_ref[...]
    solved_f = dot(prec, fine)
    fine_t = fine.T
    ff = dot(fine_t, solved_f)
    ff_ref[...] = ff
    pl.semaphore_wait(barrier, (n_leaf - 1) + (n_mid - 1) + (n_top - 1))
    ff_copies = [
        send(ff_ref, ff_in.at[step - 1], ff_send, ff_recv, "leaf", leaf, n_leaf, step)
        for step in range(1, n_leaf)
    ]
    mid_t, coarse_t = middle.T, coarse.T
    solved_m, solved_c, solved_y = dot(prec, middle), dot(prec, coarse), dot(prec, obs_ref[...])
    for place, (left_hand, right_side) in enumerate((
        (mid_t, solved_f), (coarse_t, solved_f), (fine_t, solved_y),
        (mid_t, solved_m), (mid_t, solved_c), (mid_t, solved_y),
        (coarse_t, solved_c), (coarse_t, solved_y),
    )):
        bulk_ref[:, place * r : (place + 1) * r] = dot(left_hand, right_side)
    rs_copies = []
    for step in range(1, n_leaf):
        target = lax.rem(leaf + step, n_leaf)
        rs_copies.append(send(
            bulk_ref.at[pl.ds(pl.multiple_of(target * rows, rows), rows), :], rs_in.at[step - 1],
            rs_send, rs_recv, "leaf", leaf, n_leaf, step,
        ))
    own_rows = pl.ds(pl.multiple_of(leaf * rows, rows), rows)

    total = core_fine_ref[...] + ff
    for step in range(1, n_leaf):
        ff_copies[step - 1].wait()
        total = total + ff_in[step - 1]
    fine_inverse = negated_inverse(a_ref, total)

    part = bulk_ref[own_rows, :]
    for step in range(1, n_leaf):
        rs_copies[step - 1].wait()
        part = part + rs_in[step - 1]
    quarter_ref[...] = part[:, : 3 * r]
    ag_copies = [
        send(quarter_ref, ag_ref.at[own_rows, :], ag_send, ag_recv, "leaf", leaf, n_leaf, step)
        for step in range(1, n_leaf)
    ]
    ag_ref[own_rows, :] = part[:, : 3 * r]
    for copy in ag_copies:
        copy.wait()
    w_m = dot(fine_inverse, ag_ref[:, :r].T)
    w_c = dot(fine_inverse, ag_ref[:, r : 2 * r].T)
    w_y = dot(fine_inverse, ag_ref[:, 2 * r : 3 * r])
    q_m, q_c = part[:, :r], part[:, r : 2 * r]
    for place, (left_hand, right_side) in enumerate((
        (q_m, w_m), (q_m, w_c), (q_m, w_y), (q_c, w_c), (q_c, w_y),
    )):
        piece_ref[:, place * r : (place + 1) * r] = (
            part[:, (3 + place) * r : (4 + place) * r] + dot(left_hand, right_side)
        )
    mid_copies = [
        send(piece_ref, piece_in.at[step - 1], mid_send, mid_recv, "mid", mid, n_mid, step)
        for step in range(1, n_mid)
    ]
    piece = piece_ref[...]
    for step in range(1, n_mid):
        mid_copies[step - 1].wait()
        piece = piece + piece_in[step - 1]
    piece_ref[...] = piece
    s_copies = [
        send(piece_ref, s_ref.at[own_rows, :], s_send, s_recv, "leaf", leaf, n_leaf, step)
        for step in range(1, n_leaf)
    ]
    s_ref[own_rows, :] = piece
    for copy in s_copies:
        copy.wait()

    mid_inverse = negated_inverse(a_ref, core_mid_ref[...] + s_ref[:, :r])
    cross = s_ref[:, r : 2 * r]
    v_c, v_y = dot(mid_inverse, cross), dot(mid_inverse, s_ref[:, 2 * r : 3 * r])
    cross_t = cross.T
    cc = s_ref[:, 3 * r : 4 * r] + dot(cross_t, v_c)
    cy = s_ref[:, 4 * r : 5 * r] + dot(cross_t, v_y)
    top_ref[:, :r] = cc
    top_ref[:, r:] = cy
    top_copies = [
        send(top_ref, top_in.at[step - 1], top_send, top_recv, "top", top, n_top, step)
        for step in range(1, n_top)
    ]
    for step in range(1, n_top):
        top_copies[step - 1].wait()
        cc = cc + top_in[step - 1, :, :r]
        cy = cy + top_in[step - 1, :, r:]
    coarse_inverse = negated_inverse(a_ref, core_coarse_ref[...] + cc)
    x_c = -dot(coarse_inverse, cy)
    x_m = dot(v_c, x_c) - v_y
    x_f = dot(w_m, x_m) + dot(w_c, x_c) - w_y
    out_ref[...] = solved_y - dot(solved_f, x_f) - dot(solved_m, x_m) - dot(solved_c, x_c)


def local(n_leaf, n_mid, n_top, *operands):
    blocks = [x.reshape(x.shape[-2:]) for x in operands]
    r = blocks[1].shape[1]
    rows = r // n_leaf
    f32 = jnp.float32
    dma = pltpu.SemaphoreType.DMA
    answer = pl.pallas_call(
        functools.partial(kernel, n_leaf, n_mid, n_top),
        out_shape=jax.ShapeDtypeStruct(blocks[-1].shape, f32),
        in_specs=[pl.BlockSpec(memory_space=pltpu.VMEM)] * len(blocks),
        out_specs=pl.BlockSpec(memory_space=pltpu.VMEM),
        scratch_shapes=[
            pltpu.VMEM((r + 2 * PANEL, r), f32),
            pltpu.VMEM((r, r), f32),
            pltpu.VMEM((n_leaf - 1, r, r), f32),
            pltpu.VMEM((r, 8 * r), f32),
            pltpu.VMEM((n_leaf - 1, rows, 8 * r), f32),
            pltpu.VMEM((r, 3 * r), f32),
            pltpu.VMEM((rows, 5 * r), f32),
            pltpu.VMEM((n_mid - 1, rows, 5 * r), f32),
            pltpu.VMEM((rows, 3 * r), f32),
            pltpu.VMEM((r, 5 * r), f32),
            pltpu.VMEM((r, 2 * r), f32),
            pltpu.VMEM((n_top - 1, r, 2 * r), f32),
            dma((n_leaf - 1,)), dma((n_leaf - 1,)),
            dma((n_leaf - 1,)), dma((n_leaf - 1,)),
            dma((n_leaf - 1,)), dma((n_leaf - 1,)),
            dma((n_mid - 1,)), dma((n_mid - 1,)),
            dma((n_leaf - 1,)), dma((n_leaf - 1,)),
            dma((n_top - 1,)), dma((n_top - 1,)),
        ],
        compiler_params=pltpu.CompilerParams(collective_id=0, has_side_effects=True),
    )(*blocks)
    return answer[None, None, None]


def solution(mesh):
    spread = P(("parts", "leaf"), "mid", "top", None, None)
    sizes = (mesh.shape["leaf"], mesh.shape["mid"], mesh.shape["top"])
    return jax.shard_map(
        functools.partial(local, *sizes),
        mesh=mesh,
        in_specs=(spread, spread, spread, spread, P(), P(), P(), spread),
        out_specs=spread,
        check_vma=False,
    )
```

time: 183 us -> 55.3 us (0.30)
  waiting for transfers between devices: 81.9 us -> 0 us
  other arithmetic: 71.1 us -> 0 us
  Pallas kernels: 0 us -> 53.6 us
  between operations: 13.4 us -> 0.01 us
  matrix products: 10.7 us -> 0 us
  local copies, waits for them, and re-layouts: 4.69 us -> 1.47 us
    psum x3 -> x0, waiting for transfers between devices: 81.8 us -> none  [the longest x1 41.6 us: local(): lax.psum((fine_part, mid_part, coarse_part), 'leaf')]
    another operation x15 -> x0, other arithmetic: 68.6 us -> none  [the longest x9 37.2 us: solve_core(): jnp.linalg.cholesky(matrix)]
    pallas_call x0 -> x1, Pallas kernels: none -> 53.6 us  [local(): pl.pallas_call(functools.partial(kernel, n_leaf, n_mid, n_top), out_shape...]
    dot_general x10 -> x0, matrix products: 8.93 us -> none  [the longest x6 6.2 us: cross_dot(): return jnp.dot(left_hand.T, right_side, precision=lax.Precision.HIGHEST)]
    add x3 -> x0, other arithmetic: 2.54 us -> none  [the longest x1 0.85 us: local(): core_fine + fine_gram[:, :core_rank]]
    unnamed x29 -> x1, local copies, waits for them, and re-layouts: 3.7 us -> 1.47 us
  transfers between devices with their start and end apart: 3 -> 0, of which waited for: 3 -> 0; matrix products, arithmetic and copies ran while one was open for 1% -> 0% of each run, Pallas kernels for 0% -> 0%
where the time goes in v1:
time: 55.3 us; the launch traced here: 55.1 us
  Pallas kernels  53.6 us (97%)
  local copies, waits for them, and re-layouts  1.47 us (3%)
    pallas_call x1, Pallas kernels, local(): pl.pallas_call(functools.partial(kernel, n_leaf, n_mid, n_top), out_shape...  53.6 us
    unnamed x1, local copies, waits for them, and re-layouts  1.47 us

profile of v1, /device:TPU:0, one launch (start us, length us, event | category | flops | bytes accessed | tf_op | source)
XLA Modules:
  0.0 55.1 jit_solution(636044791906612199)
XLA Ops:
  0.0 53.6 %shard_map.82 = f32[128,128]{1,0:T(8,128)} custom-call(f32[128,128]{1,0:T(8,128)} %bitcast.7, f32[128,128]{1,0:T(8,128)} %bitcast.8, f32[128,128]{1,0:T(8,128)} %bitcast.9, f32[128,128]{1,0:T(8,128)} %bitcast.10, f32[128,128]{1,0:T(8,128)} %core_fine_ref.1, f32[128,128]{1,0:T(8,128)} %core_mid_ref.1, f32[128,128]{1,0:T(8,128)} %core_coarse_ref.1, ...), custom_call_target="tpu_custom_call" | custom-call | tf_op jit(solution)/shard_map/pallas_call | solution.py:226
  53.6 1.5 %copy.10 = f32[1,1,1,128,128]{4,3,2,1,0:T(8,128)} copy(f32[1,1,1,128,128]{4,3,2,1,0:T(8,128)} %bitcast.6) | data formatting | bytes 131072

commit v2 on v1

v2 whole, which is shorter than its diff:
```python
import functools

import jax
import jax.numpy as jnp
from jax import lax
from jax.experimental import pallas as pl
from jax.experimental.pallas import tpu as pltpu
from jax.sharding import PartitionSpec as P

MESH = pl.DeviceIdType.MESH
PANEL = 8


def dot(left_hand, right_side):
    return jnp.dot(
        left_hand, right_side, precision=lax.Precision.HIGHEST, preferred_element_type=jnp.float32
    )


def split3(x):
    high = x.astype(jnp.bfloat16).astype(jnp.float32)
    rest = x - high
    mid = rest.astype(jnp.bfloat16).astype(jnp.float32)
    low = (rest - mid).astype(jnp.bfloat16).astype(jnp.float32)
    return high, mid, low


def rank_update(panel, scaled):
    p1, p2, p3 = split3(panel)
    r1, r2, r3 = split3(scaled)
    left_hand = jnp.concatenate([p1, p1, p2, p2, p1, p3], axis=0).T.astype(jnp.bfloat16)
    right_side = jnp.concatenate([r1, r2, r1, r2, r3, r1], axis=0).astype(jnp.bfloat16)
    return jnp.dot(left_hand, right_side, preferred_element_type=jnp.float32)


def negated_inverse(a_ref, matrix):
    size = matrix.shape[0]
    zero = jnp.zeros((PANEL, size), jnp.float32)
    a_ref[pl.ds(0, PANEL), :] = zero
    a_ref[pl.ds(PANEL, size), :] = matrix
    a_ref[pl.ds(PANEL + size, PANEL), :] = zero
    lane = lax.broadcasted_iota(jnp.int32, (PANEL, size), 1)
    sub = lax.broadcasted_iota(jnp.int32, (PANEL, size), 0)
    lane_full = lax.broadcasted_iota(jnp.int32, (size, size), 1)

    def columns(block, k):
        return [
            jnp.broadcast_to(
                jnp.sum(jnp.where(lane == k * PANEL + j, block, 0.0), axis=1, keepdims=True),
                block.shape,
            )
            for j in range(PANEL)
        ]

    def apply(k, panel, scaled):
        inside = (lane_full >= k * PANEL) & (lane_full < (k + 1) * PANEL)
        current = a_ref[pl.ds(PANEL, size), :]
        a_ref[pl.ds(PANEL, size), :] = jnp.where(inside, 0.0, current) - rank_update(panel, scaled)
        a_ref[pl.ds(pl.multiple_of((k + 1) * PANEL, PANEL), PANEL), :] = scaled

    def body(k, carry):
        panel_before, scaled_before, panel = carry
        apply(k - 1, panel_before, scaled_before)
        inside = (lane >= k * PANEL) & (lane < (k + 1) * PANEL)
        cols = columns(panel, k)
        x = jnp.where(inside, jnp.where(lane - k * PANEL == sub, 1.0, 0.0), panel)
        for i in range(PANEL):
            pivot = 1.0 / jnp.broadcast_to(cols[i][i : i + 1], x.shape)
            here = sub == i

            def step(v):
                row = jnp.broadcast_to(v[i : i + 1], v.shape) * pivot
                return jnp.where(here, row, v - cols[i] * row)

            x_new = step(x)
            for j in range(i + 1, PANEL):
                cols[j] = step(cols[j])
            x = x_new
        scaled = jnp.where(inside, -x, x)
        following = a_ref[pl.ds(pl.multiple_of((k + 2) * PANEL, PANEL), PANEL), :]
        coefs = columns(following, k)
        panel_next = jnp.where(inside, 0.0, following)
        for j in range(PANEL):
            panel_next = panel_next - coefs[j] * jnp.broadcast_to(scaled[j : j + 1], x.shape)
        return panel, scaled, panel_next

    steps = size // PANEL
    panel, scaled, _ = lax.fori_loop(0, steps, body, (zero, zero, matrix[:PANEL]))
    apply(steps - 1, panel, scaled)
    return a_ref[pl.ds(PANEL, size), :]


def kernel(
    n_leaf, n_mid, n_top,
    prec_ref, fine_ref, mid_ref, coarse_ref, core_fine_ref, core_mid_ref, core_coarse_ref, obs_ref,
    out_ref,
    a_ref, bulk_ref, rs_in, part_ref, ag_ref, piece_ref, piece_in, quarter_ref, s_ref, top_ref, top_in,
    rs_send, rs_recv, ag_send, ag_recv, mid_send, mid_recv, s_send, s_recv, top_send, top_recv,
):
    r = fine_ref.shape[1]
    rows = r // n_leaf
    leaf, mid, top = lax.axis_index("leaf"), lax.axis_index("mid"), lax.axis_index("top")
    own_rows = pl.ds(pl.multiple_of(leaf * rows, rows), rows)
    barrier = pltpu.get_barrier_semaphore()
    places = {"leaf": (leaf, n_leaf), "mid": (mid, n_mid), "top": (top, n_top)}

    def peer(axis, step):
        index, count = places[axis]
        return {axis: lax.rem(index + step, count)}

    for axis in places:
        for step in range(1, places[axis][1]):
            pl.semaphore_signal(barrier, inc=1, device_id=peer(axis, step), device_id_type=MESH)

    def send(src, dst, sems, phase, axis, step):
        copy = pltpu.make_async_remote_copy(
            src_ref=src, dst_ref=dst,
            send_sem=sems[0].at[phase, step - 1], recv_sem=sems[1].at[phase, step - 1],
            device_id=peer(axis, step), device_id_type=MESH,
        )
        copy.start()
        return copy

    def span(blocks):
        return slice(blocks[0] * r, blocks[1] * r)

    def scatter(phase, blocks):
        copies = []
        for step in range(1, n_leaf):
            target = lax.rem(leaf + step, n_leaf)
            target_rows = pl.ds(pl.multiple_of(target * rows, rows), rows)
            copies.append(send(
                bulk_ref.at[target_rows, span(blocks)], rs_in.at[step - 1, :, span(blocks)],
                (rs_send, rs_recv), phase, "leaf", step,
            ))
        return copies, blocks

    def collect(handle):
        copies, blocks = handle
        total = bulk_ref[own_rows, span(blocks)]
        for step in range(1, n_leaf):
            copies[step - 1].wait()
            total = total + rs_in[step - 1, :, span(blocks)]
        return total

    def gather(source, target, sems, phase, blocks, value):
        source[:, span(blocks)] = value
        copies = [
            send(
                source.at[:, span(blocks)], target.at[own_rows, span(blocks)],
                sems, phase, "leaf", step,
            )
            for step in range(1, n_leaf)
        ]
        target[own_rows, span(blocks)] = value
        return copies

    def exchange(axis, source, target, sems, phase, blocks, value):
        source[:, span(blocks)] = value
        copies = [
            send(
                source.at[:, span(blocks)], target.at[step - 1, :, span(blocks)],
                sems, phase, axis, step,
            )
            for step in range(1, places[axis][1])
        ]
        return copies, target, blocks, value

    def add_up(handle):
        copies, target, blocks, total = handle
        for step, copy in enumerate(copies):
            copy.wait()
            total = total + target[step, :, span(blocks)]
        return total

    def wait_all(copies):
        for copy in copies:
            copy.wait()

    def put(place, value):
        bulk_ref[:, place * r : (place + 1) * r] = value

    prec = prec_ref[...]
    fine, middle, coarse = fine_ref[...], mid_ref[...], coarse_ref[...]
    solved_f = dot(prec, fine)
    fine_t = fine.T
    put(0, dot(fine_t, solved_f))
    pl.semaphore_wait(barrier, (n_leaf - 1) + (n_mid - 1) + (n_top - 1))
    rs_ff = scatter(0, (0, 1))
    mid_t, coarse_t = middle.T, coarse.T
    solved_y = dot(prec, obs_ref[...])
    put(1, dot(mid_t, solved_f))
    put(2, dot(coarse_t, solved_f))
    put(3, dot(fine_t, solved_y))
    rs_f = scatter(1, (1, 4))
    solved_m, solved_c = dot(prec, middle), dot(prec, coarse)
    put(4, dot(mid_t, solved_m))
    put(5, dot(mid_t, solved_c))
    put(6, dot(mid_t, solved_y))
    put(7, dot(coarse_t, solved_c))
    put(8, dot(coarse_t, solved_y))

    first = (ag_send, ag_recv)
    ag_ff = gather(part_ref, ag_ref, first, 0, (0, 1), collect(rs_ff))
    rs_m = scatter(2, (4, 7))
    part_f = collect(rs_f)
    ag_f = gather(part_ref, ag_ref, first, 1, (1, 4), part_f)
    rs_c = scatter(3, (7, 9))

    wait_all(ag_ff)
    fine_inverse = negated_inverse(a_ref, core_fine_ref[...] + ag_ref[:, :r])
    wait_all(ag_f)
    q_m, q_c = part_f[:, :r], part_f[:, r : 2 * r]
    w_m = dot(fine_inverse, ag_ref[:, r : 2 * r].T)
    part_m = collect(rs_m)
    between, second = (mid_send, mid_recv), (s_send, s_recv)
    x_mm = exchange("mid", piece_ref, piece_in, between, 0, (0, 1), part_m[:, :r] + dot(q_m, w_m))
    w_c = dot(fine_inverse, ag_ref[:, 2 * r : 3 * r].T)
    w_y = dot(fine_inverse, ag_ref[:, 3 * r : 4 * r])
    cross_piece = jnp.concatenate(
        [part_m[:, r : 2 * r] + dot(q_m, w_c), part_m[:, 2 * r :] + dot(q_m, w_y)], axis=1
    )
    x_mc = exchange("mid", piece_ref, piece_in, between, 1, (1, 3), cross_piece)
    ag_mm = gather(quarter_ref, s_ref, second, 0, (0, 1), add_up(x_mm))
    ag_mc = gather(quarter_ref, s_ref, second, 1, (1, 3), add_up(x_mc))
    part_c = collect(rs_c)
    coarse_piece = jnp.concatenate(
        [part_c[:, :r] + dot(q_c, w_c), part_c[:, r:] + dot(q_c, w_y)], axis=1
    )
    x_cc = exchange("mid", piece_ref, piece_in, between, 2, (3, 5), coarse_piece)
    coarse_sum = add_up(x_cc)
    ag_cc = gather(quarter_ref, s_ref, second, 2, (3, 4), coarse_sum[:, :r])
    ag_cy = gather(quarter_ref, s_ref, second, 3, (4, 5), coarse_sum[:, r:])

    wait_all(ag_mm)
    mid_inverse = negated_inverse(a_ref, core_mid_ref[...] + s_ref[:, :r])
    wait_all(ag_mc)
    cross = s_ref[:, r : 2 * r]
    cross_t = cross.T
    v_c = dot(mid_inverse, cross)
    last = (top_send, top_recv)
    cross_cc = dot(cross_t, v_c)
    wait_all(ag_cc)
    x_top = exchange("top", top_ref, top_in, last, 0, (0, 1), s_ref[:, 3 * r : 4 * r] + cross_cc)
    v_y = dot(mid_inverse, s_ref[:, 2 * r : 3 * r])
    cross_cy = dot(cross_t, v_y)
    wait_all(ag_cy)
    x_right = exchange("top", top_ref, top_in, last, 1, (1, 2), s_ref[:, 4 * r : 5 * r] + cross_cy)
    coarse_inverse = negated_inverse(a_ref, core_coarse_ref[...] + add_up(x_top))
    x_c = -dot(coarse_inverse, add_up(x_right))
    x_m = dot(v_c, x_c) - v_y
    x_f = dot(w_m, x_m) + dot(w_c, x_c) - w_y
    out_ref[...] = solved_y - dot(solved_f, x_f) - dot(solved_m, x_m) - dot(solved_c, x_c)


def local(n_leaf, n_mid, n_top, *operands):
    blocks = [x.reshape(x.shape[-2:]) for x in operands]
    r = blocks[1].shape[1]
    rows = r // n_leaf
    f32 = jnp.float32

    def pair(phases, count):
        return [pltpu.SemaphoreType.DMA((phases, count - 1))] * 2

    answer = pl.pallas_call(
        functools.partial(kernel, n_leaf, n_mid, n_top),
        out_shape=jax.ShapeDtypeStruct(blocks[-1].shape, f32),
        in_specs=[pl.BlockSpec(memory_space=pltpu.VMEM)] * len(blocks),
        out_specs=pl.BlockSpec(memory_space=pltpu.VMEM),
        scratch_shapes=[
            pltpu.VMEM((r + 2 * PANEL, r), f32),
            pltpu.VMEM((r, 9 * r), f32),
            pltpu.VMEM((n_leaf - 1, rows, 9 * r), f32),
            pltpu.VMEM((rows, 4 * r), f32),
            pltpu.VMEM((r, 4 * r), f32),
            pltpu.VMEM((rows, 5 * r), f32),
            pltpu.VMEM((n_mid - 1, rows, 5 * r), f32),
            pltpu.VMEM((rows, 5 * r), f32),
            pltpu.VMEM((r, 5 * r), f32),
            pltpu.VMEM((r, 2 * r), f32),
            pltpu.VMEM((n_top - 1, r, 2 * r), f32),
            *pair(4, n_leaf), *pair(2, n_leaf), *pair(3, n_mid), *pair(4, n_leaf), *pair(2, n_top),
        ],
        compiler_params=pltpu.CompilerParams(collective_id=0, has_side_effects=True),
    )(*blocks)
    return answer[None, None, None]


def solution(mesh):
    spread = P(("parts", "leaf"), "mid", "top", None, None)
    sizes = (mesh.shape["leaf"], mesh.shape["mid"], mesh.shape["top"])
    return jax.shard_map(
        functools.partial(local, *sizes),
        mesh=mesh,
        in_specs=(spread, spread, spread, spread, P(), P(), P(), spread),
        out_specs=spread,
        check_vma=False,
    )
```

time: 55.3 us -> 48.9 us (0.88)
  Pallas kernels: 53.6 us -> 47.2 us
    pallas_call x1, Pallas kernels: 53.6 us -> 47.2 us  [local(): pl.pallas_call(functools.partial(kernel, n_leaf, n_mid, n_top), out_shape...]
where the time goes in v2:
time: 48.9 us; the launch traced here: 48.7 us
  Pallas kernels  47.2 us (97%)
  local copies, waits for them, and re-layouts  1.47 us (3%)
    pallas_call x1, Pallas kernels, local(): pl.pallas_call(functools.partial(kernel, n_leaf, n_mid, n_top), out_shape...  47.2 us
    unnamed x1, local copies, waits for them, and re-layouts  1.47 us

profile of v2, /device:TPU:0, one launch (start us, length us, event | category | flops | bytes accessed | tf_op | source)
XLA Modules:
  0.0 48.7 jit_solution(3957019772272910783)
XLA Ops:
  0.0 47.2 %shard_map.82 = f32[128,128]{1,0:T(8,128)} custom-call(f32[128,128]{1,0:T(8,128)} %bitcast.7, f32[128,128]{1,0:T(8,128)} %bitcast.8, f32[128,128]{1,0:T(8,128)} %bitcast.9, f32[128,128]{1,0:T(8,128)} %bitcast.10, f32[128,128]{1,0:T(8,128)} %core_fine_ref.1, f32[128,128]{1,0:T(8,128)} %core_mid_ref.1, f32[128,128]{1,0:T(8,128)} %core_coarse_ref.1, ...), custom_call_target="tpu_custom_call" | custom-call | tf_op jit(solution)/shard_map/pallas_call | solution.py:265
  47.2 1.5 %copy.10 = f32[1,1,1,128,128]{4,3,2,1,0:T(8,128)} copy(f32[1,1,1,128,128]{4,3,2,1,0:T(8,128)} %bitcast.6) | data formatting | bytes 131072

commit v3 on v2

--- a/solution.py
+++ b/solution.py
@@ -25,12 +25,15 @@
     return high, mid, low
 
 
-def rank_update(panel, scaled):
+def spread_panel(panel):
     p1, p2, p3 = split3(panel)
+    return jnp.concatenate([p1, p1, p2, p2, p1, p3], axis=0).T.astype(jnp.bfloat16)
+
+
+def rank_update(spread, scaled):
     r1, r2, r3 = split3(scaled)
-    left_hand = jnp.concatenate([p1, p1, p2, p2, p1, p3], axis=0).T.astype(jnp.bfloat16)
     right_side = jnp.concatenate([r1, r2, r1, r2, r3, r1], axis=0).astype(jnp.bfloat16)
-    return jnp.dot(left_hand, right_side, preferred_element_type=jnp.float32)
+    return jnp.dot(spread, right_side, preferred_element_type=jnp.float32)
 
 
 def negated_inverse(a_ref, matrix):
@@ -52,17 +55,29 @@
             for j in range(PANEL)
         ]
 
-    def apply(k, panel, scaled):
+    def apply(k, spread, scaled):
         inside = (lane_full >= k * PANEL) & (lane_full < (k + 1) * PANEL)
         current = a_ref[pl.ds(PANEL, size), :]
-        a_ref[pl.ds(PANEL, size), :] = jnp.where(inside, 0.0, current) - rank_update(panel, scaled)
+        a_ref[pl.ds(PANEL, size), :] = jnp.where(inside, 0.0, current) - rank_update(spread, scaled)
         a_ref[pl.ds(pl.multiple_of((k + 1) * PANEL, PANEL), PANEL), :] = scaled
 
     def body(k, carry):
-        panel_before, scaled_before, panel = carry
-        apply(k - 1, panel_before, scaled_before)
+        spread_before, scaled_before, panel = carry
+        apply(k - 1, spread_before, scaled_before)
+        spread = spread_panel(panel)
         inside = (lane >= k * PANEL) & (lane < (k + 1) * PANEL)
         cols = columns(panel, k)
+        ahead = lane == (k + 1) * PANEL + sub
+        coefs = [
+            jnp.broadcast_to(
+                jnp.sum(
+                    jnp.where(ahead, jnp.broadcast_to(panel[j : j + 1], panel.shape), 0.0),
+                    axis=1, keepdims=True,
+                ),
+                panel.shape,
+            )
+            for j in range(PANEL)
+        ]
         x = jnp.where(inside, jnp.where(lane - k * PANEL == sub, 1.0, 0.0), panel)
         for i in range(PANEL):
             pivot = 1.0 / jnp.broadcast_to(cols[i][i : i + 1], x.shape)
@@ -78,15 +93,14 @@
             x = x_new
         scaled = jnp.where(inside, -x, x)
         following = a_ref[pl.ds(pl.multiple_of((k + 2) * PANEL, PANEL), PANEL), :]
-        coefs = columns(following, k)
         panel_next = jnp.where(inside, 0.0, following)
         for j in range(PANEL):
             panel_next = panel_next - coefs[j] * jnp.broadcast_to(scaled[j : j + 1], x.shape)
-        return panel, scaled, panel_next
+        return spread, scaled, panel_next
 
     steps = size // PANEL
-    panel, scaled, _ = lax.fori_loop(0, steps, body, (zero, zero, matrix[:PANEL]))
-    apply(steps - 1, panel, scaled)
+    spread, scaled, _ = lax.fori_loop(0, steps, body, (spread_panel(zero), zero, matrix[:PANEL]))
+    apply(steps - 1, spread, scaled)
     return a_ref[pl.ds(PANEL, size), :]
 
 
@@ -104,6 +118,8 @@
     barrier = pltpu.get_barrier_semaphore()
     places = {"leaf": (leaf, n_leaf), "mid": (mid, n_mid), "top": (top, n_top)}
 
+    far_first = sorted(range(1, n_leaf), key=lambda step: (abs(2 * step - n_leaf), step))
+
     def peer(axis, step):
         index, count = places[axis]
         return {axis: lax.rem(index + step, count)}
@@ -125,21 +141,21 @@
         return slice(blocks[0] * r, blocks[1] * r)
 
     def scatter(phase, blocks):
-        copies = []
-        for step in range(1, n_leaf):
+        copies = {}
+        for step in far_first:
             target = lax.rem(leaf + step, n_leaf)
             target_rows = pl.ds(pl.multiple_of(target * rows, rows), rows)
-            copies.append(send(
+            copies[step] = send(
                 bulk_ref.at[target_rows, span(blocks)], rs_in.at[step - 1, :, span(blocks)],
                 (rs_send, rs_recv), phase, "leaf", step,
-            ))
+            )
         return copies, blocks
 
     def collect(handle):
         copies, blocks = handle
         total = bulk_ref[own_rows, span(blocks)]
         for step in range(1, n_leaf):
-            copies[step - 1].wait()
+            copies[step].wait()
             total = total + rs_in[step - 1, :, span(blocks)]
         return total
 
@@ -150,7 +166,7 @@
                 source.at[:, span(blocks)], target.at[own_rows, span(blocks)],
                 sems, phase, "leaf", step,
             )
-            for step in range(1, n_leaf)
+            for step in far_first
         ]
         target[own_rows, span(blocks)] = value
         return copies

time: 48.9 us -> 44.5 us (0.910)
  Pallas kernels: 47.2 us -> 42.8 us
    pallas_call x1, Pallas kernels: 47.2 us -> 42.8 us  [local(): pl.pallas_call(functools.partial(kernel, n_leaf, n_mid, n_top), out_shape...]
where the time goes in v3:
time: 44.5 us; the launch traced here: 44.3 us
  Pallas kernels  42.8 us (96%)
  local copies, waits for them, and re-layouts  1.47 us (3%)
    pallas_call x1, Pallas kernels, local(): pl.pallas_call(functools.partial(kernel, n_leaf, n_mid, n_top), out_shape...  42.8 us
    unnamed x1, local copies, waits for them, and re-layouts  1.47 us

profile of v3, /device:TPU:0, one launch (start us, length us, event | category | flops | bytes accessed | tf_op | source)
XLA Modules:
  0.0 44.3 jit_solution(12145792210018006375)
XLA Ops:
  0.0 42.8 %shard_map.82 = f32[128,128]{1,0:T(8,128)} custom-call(f32[128,128]{1,0:T(8,128)} %bitcast.7, f32[128,128]{1,0:T(8,128)} %bitcast.8, f32[128,128]{1,0:T(8,128)} %bitcast.9, f32[128,128]{1,0:T(8,128)} %bitcast.10, f32[128,128]{1,0:T(8,128)} %core_fine_ref.1, f32[128,128]{1,0:T(8,128)} %core_mid_ref.1, f32[128,128]{1,0:T(8,128)} %core_coarse_ref.1, ...), custom_call_target="tpu_custom_call" | custom-call | tf_op jit(solution)/shard_map/pallas_call | solution.py:281
  42.8 1.5 %copy.10 = f32[1,1,1,128,128]{4,3,2,1,0:T(8,128)} copy(f32[1,1,1,128,128]{4,3,2,1,0:T(8,128)} %bitcast.6) | data formatting | bytes 131072

commit v4 on v3

--- a/solution.py
+++ b/solution.py
@@ -108,8 +108,8 @@
     n_leaf, n_mid, n_top,
     prec_ref, fine_ref, mid_ref, coarse_ref, core_fine_ref, core_mid_ref, core_coarse_ref, obs_ref,
     out_ref,
-    a_ref, bulk_ref, rs_in, part_ref, ag_ref, piece_ref, piece_in, quarter_ref, s_ref, top_ref, top_in,
-    rs_send, rs_recv, ag_send, ag_recv, mid_send, mid_recv, s_send, s_recv, top_send, top_recv,
+    a_ref, bulk_ref, rs_in, pair_in, cross_ref, cross_in, part_ref, ag_ref, piece_ref, piece_in, quarter_ref, s_ref, top_ref, top_in,
+    rs_send, rs_recv, pair_send, pair_recv, cross_send, cross_recv, ag_send, ag_recv, mid_send, mid_recv, s_send, s_recv, top_send, top_recv,
 ):
     r = fine_ref.shape[1]
     rows = r // n_leaf
@@ -157,6 +157,58 @@
         for step in range(1, n_leaf):
             copies[step].wait()
             total = total + rs_in[step - 1, :, span(blocks)]
+        return total
+
+    half = n_leaf // 2
+    parity = lax.rem(leaf, 2)
+
+    def row_block(index):
+        return pl.ds(pl.multiple_of(index * rows, rows), rows)
+
+    def shifted(blocks):
+        return slice((blocks[0] - 4) * r, (blocks[1] - 4) * r)
+
+    def pair_scatter(phase, blocks):
+        copies = []
+        for j in range(half):
+            copy = pltpu.make_async_remote_copy(
+                src_ref=bulk_ref.at[row_block(2 * j + 1 - parity), span(blocks)],
+                dst_ref=pair_in.at[j, :, shifted(blocks)],
+                send_sem=pair_send.at[phase, j], recv_sem=pair_recv.at[phase, j],
+                device_id={"leaf": leaf + 1 - 2 * parity}, device_id_type=MESH,
+            )
+            copy.start()
+            copies.append(copy)
+        return copies
+
+    def cross_scatter(phase, blocks, pair_copies):
+        for copy in pair_copies:
+            copy.wait()
+        columns = shifted(blocks)
+        copies = []
+        for step in range(1, half):
+            target = lax.rem(leaf + 2 * step, n_leaf)
+            cross_ref[step - 1, :, columns] = (
+                bulk_ref[row_block(target), span(blocks)]
+                + pair_in[lax.div(target, 2), :, columns]
+            )
+            copy = pltpu.make_async_remote_copy(
+                src_ref=cross_ref.at[step - 1, :, columns],
+                dst_ref=cross_in.at[step - 1, :, columns],
+                send_sem=cross_send.at[phase, step - 1], recv_sem=cross_recv.at[phase, step - 1],
+                device_id={"leaf": target}, device_id_type=MESH,
+            )
+            copy.start()
+            copies.append(copy)
+        return copies, blocks
+
+    def cross_collect(handle):
+        copies, blocks = handle
+        columns = shifted(blocks)
+        total = bulk_ref[own_rows, span(blocks)] + pair_in[lax.div(leaf, 2), :, columns]
+        for step, copy in enumerate(copies):
+            copy.wait()
+            total = total + cross_in[step, :, columns]
         return total
 
     def gather(source, target, sems, phase, blocks, value):
@@ -218,17 +270,19 @@
 
     first = (ag_send, ag_recv)
     ag_ff = gather(part_ref, ag_ref, first, 0, (0, 1), collect(rs_ff))
-    rs_m = scatter(2, (4, 7))
+    pair_m = pair_scatter(0, (4, 7))
     part_f = collect(rs_f)
     ag_f = gather(part_ref, ag_ref, first, 1, (1, 4), part_f)
-    rs_c = scatter(3, (7, 9))
+    pair_c = pair_scatter(1, (7, 9))
+    rs_m = cross_scatter(0, (4, 7), pair_m)
 
     wait_all(ag_ff)
     fine_inverse = negated_inverse(a_ref, core_fine_ref[...] + ag_ref[:, :r])
+    rs_c = cross_scatter(1, (7, 9), pair_c)
     wait_all(ag_f)
     q_m, q_c = part_f[:, :r], part_f[:, r : 2 * r]
     w_m = dot(fine_inverse, ag_ref[:, r : 2 * r].T)
-    part_m = collect(rs_m)
+    part_m = cross_collect(rs_m)
     between, second = (mid_send, mid_recv), (s_send, s_recv)
     x_mm = exchange("mid", piece_ref, piece_in, between, 0, (0, 1), part_m[:, :r] + dot(q_m, w_m))
     w_c = dot(fine_inverse, ag_ref[:, 2 * r : 3 * r].T)
@@ -239,7 +293,7 @@
     x_mc = exchange("mid", piece_ref, piece_in, between, 1, (1, 3), cross_piece)
     ag_mm = gather(quarter_ref, s_ref, second, 0, (0, 1), add_up(x_mm))
     ag_mc = gather(quarter_ref, s_ref, second, 1, (1, 3), add_up(x_mc))
-    part_c = collect(rs_c)
+    part_c = cross_collect(rs_c)
     coarse_piece = jnp.concatenate(
         [part_c[:, :r] + dot(q_c, w_c), part_c[:, r:] + dot(q_c, w_y)], axis=1
     )
@@ -273,6 +327,7 @@
     blocks = [x.reshape(x.shape[-2:]) for x in operands]
     r = blocks[1].shape[1]
     rows = r // n_leaf
+    half = n_leaf // 2
     f32 = jnp.float32
 
     def pair(phases, count):
@@ -286,7 +341,10 @@
         scratch_shapes=[
             pltpu.VMEM((r + 2 * PANEL, r), f32),
             pltpu.VMEM((r, 9 * r), f32),
-            pltpu.VMEM((n_leaf - 1, rows, 9 * r), f32),
+            pltpu.VMEM((n_leaf - 1, rows, 4 * r), f32),
+            pltpu.VMEM((half, rows, 5 * r), f32),
+            pltpu.VMEM((half - 1, rows, 5 * r), f32),
+            pltpu.VMEM((half - 1, rows, 5 * r), f32),
             pltpu.VMEM((rows, 4 * r), f32),
             pltpu.VMEM((r, 4 * r), f32),
             pltpu.VMEM((rows, 5 * r), f32),
@@ -295,7 +353,7 @@
             pltpu.VMEM((r, 5 * r), f32),
             pltpu.VMEM((r, 2 * r), f32),
             pltpu.VMEM((n_top - 1, r, 2 * r), f32),
-            *pair(4, n_leaf), *pair(2, n_leaf), *pair(3, n_mid), *pair(4, n_leaf), *pair(2, n_top),
+            *pair(2, n_leaf), *pair(2, half + 1), *pair(2, half), *pair(2, n_leaf), *pair(3, n_mid), *pair(4, n_leaf), *pair(2, n_top),
         ],
         compiler_params=pltpu.CompilerParams(collective_id=0, has_side_effects=True),
     )(*blocks)

time: 44.5 us -> 39.9 us (0.90)
  Pallas kernels: 42.8 us -> 38.2 us
    pallas_call x1, Pallas kernels: 42.8 us -> 38.2 us  [local(): pl.pallas_call(functools.partial(kernel, n_leaf, n_mid, n_top), out_shape...]
where the time goes in v4:
time: 39.9 us; the launch traced here: 39.7 us
  Pallas kernels  38.2 us (96%)
  local copies, waits for them, and re-layouts  1.47 us (4%)
    pallas_call x1, Pallas kernels, local(): pl.pallas_call(functools.partial(kernel, n_leaf, n_mid, n_top), out_shape...  38.2 us
    unnamed x1, local copies, waits for them, and re-layouts  1.47 us

profile of v4, /device:TPU:0, one launch (start us, length us, event | category | flops | bytes accessed | tf_op | source)
XLA Modules:
  0.0 39.7 jit_solution(7861834367038829257)
XLA Ops:
  0.0 38.2 %shard_map.82 = f32[128,128]{1,0:T(8,128)} custom-call(f32[128,128]{1,0:T(8,128)} %bitcast.7, f32[128,128]{1,0:T(8,128)} %bitcast.8, f32[128,128]{1,0:T(8,128)} %bitcast.9, f32[128,128]{1,0:T(8,128)} %bitcast.10, f32[128,128]{1,0:T(8,128)} %core_fine_ref.1, f32[128,128]{1,0:T(8,128)} %core_mid_ref.1, f32[128,128]{1,0:T(8,128)} %core_coarse_ref.1, ...), custom_call_target="tpu_custom_call" | custom-call | tf_op jit(solution)/shard_map/pallas_call | solution.py:336
  38.2 1.5 %copy.10 = f32[1,1,1,128,128]{4,3,2,1,0:T(8,128)} copy(f32[1,1,1,128,128]{4,3,2,1,0:T(8,128)} %bitcast.6) | data formatting | bytes 131072

commit v5 on v4

--- a/solution.py
+++ b/solution.py
@@ -272,26 +272,28 @@
     ag_ff = gather(part_ref, ag_ref, first, 0, (0, 1), collect(rs_ff))
     pair_m = pair_scatter(0, (4, 7))
     part_f = collect(rs_f)
-    ag_f = gather(part_ref, ag_ref, first, 1, (1, 4), part_f)
+    ag_mf = gather(part_ref, ag_ref, first, 1, (1, 2), part_f[:, :r])
+    ag_f = gather(part_ref, ag_ref, first, 2, (2, 4), part_f[:, r:])
     pair_c = pair_scatter(1, (7, 9))
     rs_m = cross_scatter(0, (4, 7), pair_m)
 
     wait_all(ag_ff)
     fine_inverse = negated_inverse(a_ref, core_fine_ref[...] + ag_ref[:, :r])
     rs_c = cross_scatter(1, (7, 9), pair_c)
-    wait_all(ag_f)
+    wait_all(ag_mf)
     q_m, q_c = part_f[:, :r], part_f[:, r : 2 * r]
     w_m = dot(fine_inverse, ag_ref[:, r : 2 * r].T)
     part_m = cross_collect(rs_m)
     between, second = (mid_send, mid_recv), (s_send, s_recv)
     x_mm = exchange("mid", piece_ref, piece_in, between, 0, (0, 1), part_m[:, :r] + dot(q_m, w_m))
+    ag_mm = gather(quarter_ref, s_ref, second, 0, (0, 1), add_up(x_mm))
+    wait_all(ag_f)
     w_c = dot(fine_inverse, ag_ref[:, 2 * r : 3 * r].T)
     w_y = dot(fine_inverse, ag_ref[:, 3 * r : 4 * r])
     cross_piece = jnp.concatenate(
         [part_m[:, r : 2 * r] + dot(q_m, w_c), part_m[:, 2 * r :] + dot(q_m, w_y)], axis=1
     )
     x_mc = exchange("mid", piece_ref, piece_in, between, 1, (1, 3), cross_piece)
-    ag_mm = gather(quarter_ref, s_ref, second, 0, (0, 1), add_up(x_mm))
     ag_mc = gather(quarter_ref, s_ref, second, 1, (1, 3), add_up(x_mc))
     part_c = cross_collect(rs_c)
     coarse_piece = jnp.concatenate(
@@ -353,7 +355,7 @@
             pltpu.VMEM((r, 5 * r), f32),
             pltpu.VMEM((r, 2 * r), f32),
             pltpu.VMEM((n_top - 1, r, 2 * r), f32),
-            *pair(2, n_leaf), *pair(2, half + 1), *pair(2, half), *pair(2, n_leaf), *pair(3, n_mid), *pair(4, n_leaf), *pair(2, n_top),
+            *pair(2, n_leaf), *pair(2, half + 1), *pair(2, half), *pair(3, n_leaf), *pair(3, n_mid), *pair(4, n_leaf), *pair(2, n_top),
         ],
         compiler_params=pltpu.CompilerParams(collective_id=0, has_side_effects=True),
     )(*blocks)

time: 39.9 us -> 42.8 us (1.073)
  Pallas kernels: 38.2 us -> 41.1 us
    pallas_call x1, Pallas kernels: 38.2 us -> 41.1 us  [local(): pl.pallas_call(functools.partial(kernel, n_leaf, n_mid, n_top), out_shape...]
where the time goes in v5:
time: 42.8 us; the launch traced here: 42.5 us
  Pallas kernels  41.1 us (96%)
  local copies, waits for them, and re-layouts  1.47 us (3%)
    pallas_call x1, Pallas kernels, local(): pl.pallas_call(functools.partial(kernel, n_leaf, n_mid, n_top), out_shape...  41.1 us
    unnamed x1, local copies, waits for them, and re-layouts  1.47 us

profile of v5, /device:TPU:0, one launch (start us, length us, event | category | flops | bytes accessed | tf_op | source)
XLA Modules:
  0.0 42.5 jit_solution(15604357379898257327)
XLA Ops:
  0.0 41.1 %shard_map.82 = f32[128,128]{1,0:T(8,128)} custom-call(f32[128,128]{1,0:T(8,128)} %bitcast.7, f32[128,128]{1,0:T(8,128)} %bitcast.8, f32[128,128]{1,0:T(8,128)} %bitcast.9, f32[128,128]{1,0:T(8,128)} %bitcast.10, f32[128,128]{1,0:T(8,128)} %core_fine_ref.1, f32[128,128]{1,0:T(8,128)} %core_mid_ref.1, f32[128,128]{1,0:T(8,128)} %core_coarse_ref.1, ...), custom_call_target="tpu_custom_call" | custom-call | tf_op jit(solution)/shard_map/pallas_call | solution.py:338
  41.1 1.5 %copy.10 = f32[1,1,1,128,128]{4,3,2,1,0:T(8,128)} copy(f32[1,1,1,128,128]{4,3,2,1,0:T(8,128)} %bitcast.6) | data formatting | bytes 131072
